TPU v7x, 32 devices: a whole 2x2x4 slice. The times are simulated.
32 devices in a mesh: ctx: 16 (over z, y, core), tp: 2 (over x).
Axes of the slice: x: 2, y: 2, z: 4, core: 2. Of those that a mesh axis runs over, the one named last changes fastest.
Arguments:
- queries: bfloat16 [2048, 8192], P('ctx', 'tp'), may hold values from -256 to 256
- keys: bfloat16 [2048, 1024], P(('ctx', 'tp')), may hold values from -6.5 to 6.5
- values: bfloat16 [2048, 1024], P(('ctx', 'tp')), may hold values from -6 to 6
- output_gradient: bfloat16 [2048, 8192], P('ctx', 'tp'), may hold values from -6 to 6
- span_order: int32 [32], replicated, may hold values from 0 to 31, as said below
Outputs:
- query_grad: bfloat16 [2048, 8192], P('ctx', 'tp')
- key_gradient_rows: bfloat16 [2048, 1024], P(('ctx', 'tp'))
- value_gradient_rows: bfloat16 [2048, 1024], P(('ctx', 'tp'))
Inputs may be any that keep to these rules, and one draw needn't show every extreme that they name: `span_order`: each value 0 to 31 appears once; entries 2d and 2d + 1 sum to 31.
All inputs are finite; a program needn't handle non-finite values.
Results may differ from a plain program's by a relative error of at most 0.0073.
Values may be sent and summed in bfloat16 or wider, within the bound.
A program may use at most 64 MiB of HBM per device.

v0:
```python
import math

import jax
import jax.numpy as jnp
from jax import lax
from jax.sharding import PartitionSpec as P

HEAD_SIZE = 128
QUERY_HEADS = 64
KEY_VALUE_HEADS = 8


def body(queries, keys, values, output_gradient, span_order):
    scale = HEAD_SIZE ** (-0.5)
    head_group = QUERY_HEADS // KEY_VALUE_HEADS
    k_local, v_local = (
        lax.all_to_all(keys, "tp", split_axis=1, concat_axis=0, tiled=True),
        lax.all_to_all(values, "tp", split_axis=1, concat_axis=0, tiled=True),
    )
    tokens_here = queries.shape[0]
    kv_heads = k_local.shape[1] // HEAD_SIZE
    whole_k, whole_v = (
        lax.all_gather(k_local, "ctx", axis=0, tiled=True),
        lax.all_gather(v_local, "ctx", axis=0, tiled=True),
    )
    length = whole_k.shape[0]
    span = tokens_here // 2
    ctx_index = lax.axis_index("ctx")
    own_spans = lax.dynamic_slice_in_dim(span_order, 2 * ctx_index, 2)
    local_rows = jnp.arange(tokens_here, dtype=jnp.int32)
    own_pos = (
        jnp.repeat(own_spans, span, total_repeat_length=tokens_here) * span + local_rows % span
    )
    query_pos = jnp.tile(own_pos, head_group)
    all_rows = jnp.arange(length, dtype=jnp.int32)
    all_pos = jnp.repeat(span_order, span, total_repeat_length=length) * span + all_rows % span
    q_rows = (
        queries.reshape(tokens_here, kv_heads, head_group, HEAD_SIZE)
        .transpose(1, 2, 0, 3)
        .reshape(kv_heads, head_group * tokens_here, HEAD_SIZE)
    )
    g_rows = (
        output_gradient.reshape(tokens_here, kv_heads, head_group, HEAD_SIZE)
        .transpose(1, 2, 0, 3)
        .reshape(kv_heads, head_group * tokens_here, HEAD_SIZE)
    )

    def scores(k_block, pos_block):
        score = (
            jnp.einsum("gqd,gkd->gqk", q_rows, k_block, preferred_element_type=jnp.float32) * scale
        )
        return (score, query_pos[:, None] >= pos_block[None, :])

    width = math.gcd(whole_k.shape[0], 256)
    count = whole_k.shape[0] // width
    k_blocks = whole_k.reshape(count, width, kv_heads, HEAD_SIZE).transpose(0, 2, 1, 3)
    v_blocks = whole_v.reshape(count, width, kv_heads, HEAD_SIZE).transpose(0, 2, 1, 3)
    k_blocks, v_blocks, pos_blocks = (k_blocks, v_blocks, all_pos.reshape(count, width))

    def stats_step(carry, items):
        top, total = carry
        k_block, pos_block = items
        score, visible = scores(k_block, pos_block)
        score = jnp.where(visible[None], score, -1e30)
        new_top = jnp.maximum(top, jnp.max(score, axis=-1))
        expo = jnp.where(visible[None], jnp.exp(score - new_top[..., None]), 0.0)
        total = total * jnp.exp(top - new_top) + jnp.sum(expo, axis=-1)
        return ((new_top, total), None)

    start_top = jnp.full((kv_heads, head_group * tokens_here), -1e30, jnp.float32)
    start_total = jnp.zeros((kv_heads, head_group * tokens_here), jnp.float32)
    (top, total), _ = lax.scan(stats_step, (start_top, start_total), (k_blocks, pos_blocks))

    def probs(k_block, v_block, pos_block):
        score, visible = scores(k_block, pos_block)
        prob = jnp.where(visible[None], jnp.exp(score - top[..., None]), 0.0) / total[..., None]
        dprob = jnp.einsum("gqd,gkd->gqk", g_rows, v_block, preferred_element_type=jnp.float32)
        return (prob, dprob)

    def delta_step(carry, items):
        prob, dprob = probs(*items)
        return (carry + jnp.sum(prob * dprob, axis=-1), None)

    delta, _ = lax.scan(delta_step, jnp.zeros_like(total), (k_blocks, v_blocks, pos_blocks))

    def block_grads(k_block, v_block, pos_block):
        prob, dprob = probs(k_block, v_block, pos_block)
        dscore = (prob * (dprob - delta[..., None]) * scale).astype(jnp.bfloat16)
        return (prob, dscore)

    def key_value_terms(prob, dscore):
        key_gradient = jnp.einsum(
            "gqk,gqd->kgd", dscore, q_rows, preferred_element_type=jnp.float32
        )
        value_gradient = jnp.einsum(
            "gqk,gqd->kgd", prob.astype(jnp.bfloat16), g_rows, preferred_element_type=jnp.float32
        )
        return (key_gradient, value_gradient)

    start_dq = jnp.zeros((kv_heads, head_group * tokens_here, HEAD_SIZE), jnp.float32)

    def grad_step(carry, items):
        prob, dscore = block_grads(*items)
        carry = carry + jnp.einsum(
            "gqk,gkd->gqd", dscore, items[0], preferred_element_type=jnp.float32
        )
        return (carry, key_value_terms(prob, dscore))

    dquery, (dkey_terms, dvalue_terms) = lax.scan(
        grad_step, start_dq, (k_blocks, v_blocks, pos_blocks)
    )
    dkey_terms = dkey_terms.reshape(length, kv_heads * HEAD_SIZE)
    dvalue_terms = dvalue_terms.reshape(length, kv_heads * HEAD_SIZE)
    key_sum, value_sum = (
        lax.psum_scatter(dkey_terms, "ctx", scatter_dimension=0, tiled=True),
        lax.psum_scatter(dvalue_terms, "ctx", scatter_dimension=0, tiled=True),
    )
    dquery = (
        dquery.reshape(kv_heads, head_group, tokens_here, HEAD_SIZE)
        .transpose(2, 0, 1, 3)
        .reshape(tokens_here, kv_heads * head_group * HEAD_SIZE)
    )
    key_out, value_out = (
        lax.all_to_all(key_sum.astype(jnp.bfloat16), "tp", split_axis=0, concat_axis=1, tiled=True),
        lax.all_to_all(
            value_sum.astype(jnp.bfloat16), "tp", split_axis=0, concat_axis=1, tiled=True
        ),
    )
    return (dquery.astype(jnp.bfloat16), key_out, value_out)


def solution(mesh):
    return jax.shard_map(
        body,
        mesh=mesh,
        in_specs=(
            P("ctx", "tp"),
            P(("ctx", "tp"), None),
            P(("ctx", "tp"), None),
            P("ctx", "tp"),
            P(),
        ),
        out_specs=(P("ctx", "tp"), P(("ctx", "tp"), None), P(("ctx", "tp"), None)),
        check_vma=False,
    )
```

profile of v0, /device:TPU:0, one launch (start us, length us, event | category | flops | bytes accessed | tf_op | source)
XLA Modules:
  0.0 672.8 jit_solution(17401970176258699070)
XLA Ops:
  8.2 8.6 %all_to_all.76 = bf16[64,2,512]{2,0,1:T(8,128)(2,1)} all-to-all(bf16[64,2,512]{2,0,1:T(8,128)(2,1)S(1)} %bitcast.244), channel_id=1, replica_groups=mesh['ctx'=16,'tp'=2] {'tp'}, dimensions={1} | all-to-all | bytes 262144 | tf_op jit(solution)/shard_map/all_to_all | solution.py:17
  17.8 7.5 %all_to_all.77 = bf16[64,2,512]{2,0,1:T(8,128)(2,1)} all-to-all(bf16[64,2,512]{2,0,1:T(8,128)(2,1)S(1)} %bitcast.245), channel_id=1, replica_groups=mesh['ctx'=16,'tp'=2] {'tp'}, dimensions={1} | all-to-all | bytes 262144 | tf_op jit(solution)/shard_map/all_to_all | solution.py:18
  30.9 4.3 compare_select_fusion.1
  35.8 15.9 %select_multiply_fusion.1 = s32[2048]{0:T(1024)S(1)} fusion(pred[2048]{0:T(1024)(128)(4,1)S(1)} %get-tuple-element.414, pred[2048]{0:T(1024)(128)(4,1)S(1)} %get-tuple-element.413, pred[2048]{0:T(1024)(128)(4,1)S(1)} %get-tuple-element.412, pred[2048]{0:T(1024)(128)(4,1)S(1)} %get-tuple-element.411, pred[2048]{0:T(1024)(128)(4,1)S(1)} %get-tuple-element.410, ...), kind=kLoop, calls=%fused_computation.97 | loop fusion | flops 53248 | bytes 67684 | tf_op jit(solution)/shard_map/mul | solution.py:36
  63.6 38.1 %all-gather.5.cloned.1.call-done = bf16[2048,512]{1,0:T(8,128)(2,1)} async-done(((bf16[128,512]{1,0:T(8,128)(2,1)}), bf16[2048,512]{1,0:T(8,128)(2,1)}) %all-gather.5.cloned.1.call-update) | async-done | bytes 2097168 | tf_op jit(solution)/shard_map/all_gather | solution.py:24
  106.1 26.0 %while.41 = (s32[]{:T(128)}, f32[4,1024]{1,0:T(4,128)S(1)}, f32[4,1024]{1,0:T(4,128)S(1)}, s32[8,256]{1,0:T(8,128)S(1)}, bf16[8,4,256,128]{3,2,1,0:T(8,128)(2,1)...) while((s32[]{:T(128)}, f32[4,1024]{1,0:T(4,128)S(1)}, ...), condition=%wide.region_3.4_spmd.clone, body=%wide.region_0.3_spmd.clone.sunk | while | flops 277106688 | bytes 10710648 | solution.py:72
  132.1 39.0 %while.42 = (s32[]{:T(128)}, f32[4,1024]{1,0:T(4,128)S(1)}, s32[8,256]{1,0:T(8,128)S(1)}, bf16[8,4,256,128]{3,2,1,0:T(8,128)(2,1)}, bf16[4,1024,128]{2,1,0:T(8,1...) while((s32[]{:T(128)}, f32[4,1024]{1,0:T(4,128)S(1)}, ...), condition=%wide.region_6.7_spmd.clone, body=%wide.region_4.6_spmd.clone.sunk | while | flops 543428608 | bytes 11644563 | solution.py:84
  171.0 331.6 %while.43 = (s32[]{:T(128)}, f32[4,1024,128]{2,1,0:T(8,128)}, f32[8,256,4,128]{1,0,3,2:T(8,128)}, f32[8,256,4,128]{1,0,3,2:T(8,128)}, s32[8,256]{1,0:T(8,128)S(1...) while((s32[]{:T(128)}, f32[4,1024,128]{2,1,0:T(8,128)}, ...), condition=%wide.region_8.9_spmd.clone, body=%wide.region_7.8_spmd.clone.sunk | while | flops 1352925184 | bytes 33877688 | solution.py:109
  186.4 12.7 %dynamic_update_slice.11 = f32[8,256,4,128]{1,0,3,2:T(8,128)} dynamic-update-slice(f32[8,256,4,128]{1,0,3,2:T(8,128)} %get-tuple-element.782, f32[1,256,4,128]{1,0,3,2:T(1,128)S(1)} %copy.98, s32[]{:T(128)S(6)} %copy.121, s32[]{:T(128)} %constant.241.clone.1..sunk.2, s32[]{:T(128)} %constant.241.clone.1..sunk.2, s32[]{:T(128)} %constant.241.clone.1..sunk.2) | dynamic-update-slice | bytes 1048580 | tf_op jit(solution)/shard_map/while/body/jit(dynamic_update_index_in_dim)/dynamic_update_slice | solution.py:109
  199.1 12.7 %dynamic_update_slice.12 = f32[8,256,4,128]{1,0,3,2:T(8,128)} dynamic-update-slice(f32[8,256,4,128]{1,0,3,2:T(8,128)} %get-tuple-element.783, f32[1,256,4,128]{1,0,3,2:T(1,128)} %copy.99, s32[]{:T(128)S(6)} %copy.121, s32[]{:T(128)} %constant.241.clone.1..sunk.2, s32[]{:T(128)} %constant.241.clone.1..sunk.2, s32[]{:T(128)} %constant.241.clone.1..sunk.2) | dynamic-update-slice | bytes 1048580 | tf_op jit(solution)/shard_map/while/body/jit(dynamic_update_index_in_dim)/dynamic_update_slice | solution.py:109
  222.6 4.0 select_add_fusion.5
  227.9 12.7 %dynamic_update_slice.11 = f32[8,256,4,128]{1,0,3,2:T(8,128)} dynamic-update-slice(f32[8,256,4,128]{1,0,3,2:T(8,128)} %get-tuple-element.782, f32[1,256,4,128]{1,0,3,2:T(1,128)S(1)} %copy.98, s32[]{:T(128)S(6)} %copy.121, s32[]{:T(128)} %constant.241.clone.1..sunk.2, s32[]{:T(128)} %constant.241.clone.1..sunk.2, s32[]{:T(128)} %constant.241.clone.1..sunk.2) | dynamic-update-slice | bytes 1048580 | tf_op jit(solution)/shard_map/while/body/jit(dynamic_update_index_in_dim)/dynamic_update_slice | solution.py:109
  240.7 12.7 %dynamic_update_slice.12 = f32[8,256,4,128]{1,0,3,2:T(8,128)} dynamic-update-slice(f32[8,256,4,128]{1,0,3,2:T(8,128)} %get-tuple-element.783, f32[1,256,4,128]{1,0,3,2:T(1,128)} %copy.99, s32[]{:T(128)S(6)} %copy.121, s32[]{:T(128)} %constant.241.clone.1..sunk.2, s32[]{:T(128)} %constant.241.clone.1..sunk.2, s32[]{:T(128)} %constant.241.clone.1..sunk.2) | dynamic-update-slice | bytes 1048580 | tf_op jit(solution)/shard_map/while/body/jit(dynamic_update_index_in_dim)/dynamic_update_slice | solution.py:109
  264.2 4.0 select_add_fusion.5
  269.5 12.7 %dynamic_update_slice.11 = f32[8,256,4,128]{1,0,3,2:T(8,128)} dynamic-update-slice(f32[8,256,4,128]{1,0,3,2:T(8,128)} %get-tuple-element.782, f32[1,256,4,128]{1,0,3,2:T(1,128)S(1)} %copy.98, s32[]{:T(128)S(6)} %copy.121, s32[]{:T(128)} %constant.241.clone.1..sunk.2, s32[]{:T(128)} %constant.241.clone.1..sunk.2, s32[]{:T(128)} %constant.241.clone.1..sunk.2) | dynamic-update-slice | bytes 1048580 | tf_op jit(solution)/shard_map/while/body/jit(dynamic_update_index_in_dim)/dynamic_update_slice | solution.py:109
  282.2 12.7 %dynamic_update_slice.12 = f32[8,256,4,128]{1,0,3,2:T(8,128)} dynamic-update-slice(f32[8,256,4,128]{1,0,3,2:T(8,128)} %get-tuple-element.783, f32[1,256,4,128]{1,0,3,2:T(1,128)} %copy.99, s32[]{:T(128)S(6)} %copy.121, s32[]{:T(128)} %constant.241.clone.1..sunk.2, s32[]{:T(128)} %constant.241.clone.1..sunk.2, s32[]{:T(128)} %constant.241.clone.1..sunk.2) | dynamic-update-slice | bytes 1048580 | tf_op jit(solution)/shard_map/while/body/jit(dynamic_update_index_in_dim)/dynamic_update_slice | solution.py:109
  305.7 4.0 select_add_fusion.5
  311.0 12.7 %dynamic_update_slice.11 = f32[8,256,4,128]{1,0,3,2:T(8,128)} dynamic-update-slice(f32[8,256,4,128]{1,0,3,2:T(8,128)} %get-tuple-element.782, f32[1,256,4,128]{1,0,3,2:T(1,128)S(1)} %copy.98, s32[]{:T(128)S(6)} %copy.121, s32[]{:T(128)} %constant.241.clone.1..sunk.2, s32[]{:T(128)} %constant.241.clone.1..sunk.2, s32[]{:T(128)} %constant.241.clone.1..sunk.2) | dynamic-update-slice | bytes 1048580 | tf_op jit(solution)/shard_map/while/body/jit(dynamic_update_index_in_dim)/dynamic_update_slice | solution.py:109
  323.7 12.7 %dynamic_update_slice.12 = f32[8,256,4,128]{1,0,3,2:T(8,128)} dynamic-update-slice(f32[8,256,4,128]{1,0,3,2:T(8,128)} %get-tuple-element.783, f32[1,256,4,128]{1,0,3,2:T(1,128)} %copy.99, s32[]{:T(128)S(6)} %copy.121, s32[]{:T(128)} %constant.241.clone.1..sunk.2, s32[]{:T(128)} %constant.241.clone.1..sunk.2, s32[]{:T(128)} %constant.241.clone.1..sunk.2) | dynamic-update-slice | bytes 1048580 | tf_op jit(solution)/shard_map/while/body/jit(dynamic_update_index_in_dim)/dynamic_update_slice | solution.py:109
  347.3 4.0 select_add_fusion.5
  352.5 12.7 %dynamic_update_slice.11 = f32[8,256,4,128]{1,0,3,2:T(8,128)} dynamic-update-slice(f32[8,256,4,128]{1,0,3,2:T(8,128)} %get-tuple-element.782, f32[1,256,4,128]{1,0,3,2:T(1,128)S(1)} %copy.98, s32[]{:T(128)S(6)} %copy.121, s32[]{:T(128)} %constant.241.clone.1..sunk.2, s32[]{:T(128)} %constant.241.clone.1..sunk.2, s32[]{:T(128)} %constant.241.clone.1..sunk.2) | dynamic-update-slice | bytes 1048580 | tf_op jit(solution)/shard_map/while/body/jit(dynamic_update_index_in_dim)/dynamic_update_slice | solution.py:109
  365.3 12.7 %dynamic_update_slice.12 = f32[8,256,4,128]{1,0,3,2:T(8,128)} dynamic-update-slice(f32[8,256,4,128]{1,0,3,2:T(8,128)} %get-tuple-element.783, f32[1,256,4,128]{1,0,3,2:T(1,128)} %copy.99, s32[]{:T(128)S(6)} %copy.121, s32[]{:T(128)} %constant.241.clone.1..sunk.2, s32[]{:T(128)} %constant.241.clone.1..sunk.2, s32[]{:T(128)} %constant.241.clone.1..sunk.2) | dynamic-update-slice | bytes 1048580 | tf_op jit(solution)/shard_map/while/body/jit(dynamic_update_index_in_dim)/dynamic_update_slice | solution.py:109
  394.1 12.7 %dynamic_update_slice.11 = f32[8,256,4,128]{1,0,3,2:T(8,128)} dynamic-update-slice(f32[8,256,4,128]{1,0,3,2:T(8,128)} %get-tuple-element.782, f32[1,256,4,128]{1,0,3,2:T(1,128)S(1)} %copy.98, s32[]{:T(128)S(6)} %copy.121, s32[]{:T(128)} %constant.241.clone.1..sunk.2, s32[]{:T(128)} %constant.241.clone.1..sunk.2, s32[]{:T(128)} %constant.241.clone.1..sunk.2) | dynamic-update-slice | bytes 1048580 | tf_op jit(solution)/shard_map/while/body/jit(dynamic_update_index_in_dim)/dynamic_update_slice | solution.py:109
  406.8 12.7 %dynamic_update_slice.12 = f32[8,256,4,128]{1,0,3,2:T(8,128)} dynamic-update-slice(f32[8,256,4,128]{1,0,3,2:T(8,128)} %get-tuple-element.783, f32[1,256,4,128]{1,0,3,2:T(1,128)} %copy.99, s32[]{:T(128)S(6)} %copy.121, s32[]{:T(128)} %constant.241.clone.1..sunk.2, s32[]{:T(128)} %constant.241.clone.1..sunk.2, s32[]{:T(128)} %constant.241.clone.1..sunk.2) | dynamic-update-slice | bytes 1048580 | tf_op jit(solution)/shard_map/while/body/jit(dynamic_update_index_in_dim)/dynamic_update_slice | solution.py:109
  435.6 12.7 %dynamic_update_slice.11 = f32[8,256,4,128]{1,0,3,2:T(8,128)} dynamic-update-slice(f32[8,256,4,128]{1,0,3,2:T(8,128)} %get-tuple-element.782, f32[1,256,4,128]{1,0,3,2:T(1,128)S(1)} %copy.98, s32[]{:T(128)S(6)} %copy.121, s32[]{:T(128)} %constant.241.clone.1..sunk.2, s32[]{:T(128)} %constant.241.clone.1..sunk.2, s32[]{:T(128)} %constant.241.clone.1..sunk.2) | dynamic-update-slice | bytes 1048580 | tf_op jit(solution)/shard_map/while/body/jit(dynamic_update_index_in_dim)/dynamic_update_slice | solution.py:109
  448.3 12.7 %dynamic_update_slice.12 = f32[8,256,4,128]{1,0,3,2:T(8,128)} dynamic-update-slice(f32[8,256,4,128]{1,0,3,2:T(8,128)} %get-tuple-element.783, f32[1,256,4,128]{1,0,3,2:T(1,128)} %copy.99, s32[]{:T(128)S(6)} %copy.121, s32[]{:T(128)} %constant.241.clone.1..sunk.2, s32[]{:T(128)} %constant.241.clone.1..sunk.2, s32[]{:T(128)} %constant.241.clone.1..sunk.2) | dynamic-update-slice | bytes 1048580 | tf_op jit(solution)/shard_map/while/body/jit(dynamic_update_index_in_dim)/dynamic_update_slice | solution.py:109
  477.2 12.7 %dynamic_update_slice.11 = f32[8,256,4,128]{1,0,3,2:T(8,128)} dynamic-update-slice(f32[8,256,4,128]{1,0,3,2:T(8,128)} %get-tuple-element.782, f32[1,256,4,128]{1,0,3,2:T(1,128)S(1)} %copy.98, s32[]{:T(128)S(6)} %copy.121, s32[]{:T(128)} %constant.241.clone.1..sunk.2, s32[]{:T(128)} %constant.241.clone.1..sunk.2, s32[]{:T(128)} %constant.241.clone.1..sunk.2) | dynamic-update-slice | bytes 1048580 | tf_op jit(solution)/shard_map/while/body/jit(dynamic_update_index_in_dim)/dynamic_update_slice | solution.py:109
  489.9 12.7 %dynamic_update_slice.12 = f32[8,256,4,128]{1,0,3,2:T(8,128)} dynamic-update-slice(f32[8,256,4,128]{1,0,3,2:T(8,128)} %get-tuple-element.783, f32[1,256,4,128]{1,0,3,2:T(1,128)} %copy.99, s32[]{:T(128)S(6)} %copy.121, s32[]{:T(128)} %constant.241.clone.1..sunk.2, s32[]{:T(128)} %constant.241.clone.1..sunk.2, s32[]{:T(128)} %constant.241.clone.1..sunk.2) | dynamic-update-slice | bytes 1048580 | tf_op jit(solution)/shard_map/while/body/jit(dynamic_update_index_in_dim)/dynamic_update_slice | solution.py:109
  502.6 6.1 copy.85
  508.8 6.1 copy.84
  515.0 65.5 %reduce-scatter.5.cloned.1.call-done = f32[128,512]{0,1:T(8,128)} async-done(((f32[2048,512]{0,1:T(8,128)}), f32[128,512]{0,1:T(8,128)}) %reduce-scatter.5.cloned.1.call-update) | async-done | bytes 262160 | tf_op jit(solution)/shard_map/reduce_scatter | solution.py:116
  585.6 70.4 %reduce-scatter.3.cloned.1.call-done = f32[128,512]{0,1:T(8,128)} async-done(((f32[2048,512]{0,1:T(8,128)}), f32[128,512]{0,1:T(8,128)}) %reduce-scatter.3.cloned.1.call-update) | async-done | bytes 262160 | tf_op jit(solution)/shard_map/reduce_scatter | solution.py:115
  (240 shorter events, 215.3 us)
Async XLA Ops:
  7.2 46.5 %copy-start = (bf16[128,4096]{1,0:T(8,128)(2,1)S(1)}, bf16[128,4096]{1,0:T(8,128)(2,1)}, u32[]{:S(2)}) copy-start(bf16[128,4096]{1,0:T(8,128)(2,1)} %param.18) | copy-start | bytes 3145732
  7.2 52.0 %all-gather.3.cloned.1.call-start = ((), (), s32[]{:S(2)}) async-start(), calls=%async_computation.6 | async-start | bytes 2228224 | tf_op jit(solution)/shard_map/all_gather | solution.py:23
  16.9 84.8 %all-gather.5.cloned.1.call-start = ((), (), s32[]{:S(2)}) async-start(), calls=%async_computation.7 | async-start | bytes 2228224 | tf_op jit(solution)/shard_map/all_gather | solution.py:24
  25.4 555.1 %reduce-scatter.5.cloned.1.call-start = ((), (), s32[]{:S(2)}) async-start(), calls=%async_computation.9 | async-start | bytes 4456448 | tf_op jit(solution)/shard_map/reduce_scatter | solution.py:116
  51.7 4.1 copy-start.1
  508.8 147.2 %reduce-scatter.3.cloned.1.call-start = ((), (), s32[]{:S(2)}) async-start(), calls=%async_computation.8 | async-start | bytes 4456448 | tf_op jit(solution)/shard_map/reduce_scatter | solution.py:115
  582.2 75.6 %all-to-all-start.3 = ((bf16[2,64,512]{2,1,0:T(8,128)(2,1)}), bf16[2,64,512]{2,1,0:T(8,128)(2,1)S(1)}, u32[]{:S(2)}, u32[]{:S(2)}) async-start(bf16[2,64,512]{2,1,0:T(8,128)(2,1)} %bitcast.58), calls=%async_computation.5 | async-start | bytes 262144 | tf_op jit(solution)/shard_map/all_to_all | solution.py:125
  657.7 7.9 %all-to-all-start.2 = ((bf16[2,64,512]{2,1,0:T(8,128)(2,1)}), bf16[2,64,512]{2,1,0:T(8,128)(2,1)S(1)}, u32[]{:S(2)}, u32[]{:S(2)}) async-start(bf16[2,64,512]{2,1,0:T(8,128)(2,1)} %bitcast.56), calls=%async_computation.3 | async-start | bytes 262144 | tf_op jit(solution)/shard_map/all_to_all | solution.py:124
Sparse Core Ops, SparseCore 0:
  17.0 42.1 all-gather.2
  61.3 40.2 all-gather.4
  508.9 71.4 reduce-scatter.4
  584.1 71.8 reduce-scatter.2
where the time goes:
time: 681 us; the launch traced here: 673 us
  local copies, waits for them, and re-layouts  267 us (39%)
  waiting for transfers between devices  176 us (26%)
  matrix products  151 us (22%)
  other arithmetic  40.5 us (6%)
  blocking collectives  16.1 us (2%)
  between operations  14 us (2%)
  starting transfers between devices  6.92 us (1%)
    dynamic_update_slice x32, local copies, waits for them, and re-layouts, body(): lax.scan(grad_step, start_dq, (k_blocks, v_blocks, pos_blocks))  230 us
    reduce_scatter x1, waiting for transfers between devices, body(): lax.psum_scatter(dkey_terms, 'ctx', scatter_dimension=0, tiled=True)  70.4 us
    reduce_scatter x1, waiting for transfers between devices, body(): lax.psum_scatter(dvalue_terms, 'ctx', scatter_dimension=0, tiled=True)  65.5 us
    dot_general x24, matrix products, scores(): jnp.einsum('gqd,gkd->gqk', q_rows, k_block, preferred_element_type=jnp.fl...  46.2 us
    dot_general x16, matrix products, probs(): jnp.einsum('gqd,gkd->gqk', g_rows, v_block, preferred_element_type=jnp.fl...  39.7 us
    all_gather x1, waiting for transfers between devices, body(): lax.all_gather(v_local, 'ctx', axis=0, tiled=True)  38.1 us
    dot_general x8, matrix products, grad_step(): jnp.einsum('gqk,gkd->gqd', dscore, items[0], preferred_element_type=jnp.f...  31.2 us
    dot_general x8, matrix products, key_value_terms(): jnp.einsum('gqk,gqd->kgd', prob.astype(jnp.bfloat16), g_rows, preferred_e...  22.2 us
  transfers between devices with their start and end apart: 6, of which 4 were waited for; matrix products, arithmetic and copies ran while one was open for 8% of the time, Pallas kernels for 0%

commit v1 on v0

v1 whole, which is shorter than its diff:
```python
import functools
import math

import jax
import jax.numpy as jnp
from jax import lax
from jax.experimental import pallas as pl
from jax.experimental.pallas import tpu as pltpu
from jax.sharding import PartitionSpec as P

HEAD_SIZE = 128
QUERY_HEADS = 64
KEY_VALUE_HEADS = 8
GROUP = QUERY_HEADS // KEY_VALUE_HEADS
SCALE = HEAD_SIZE ** (-0.5)
LOG2E = math.log2(math.e)
NT = (((1,), (1,)), ((), ()))
F32 = jnp.float32
BF16 = jnp.bfloat16


def attention_kernel(
    order_ref, q_ref, g_ref, k_ref, v_ref, dq_ref, dk_ref, dv_ref,
    qs, gs, kseq, vseq, kt, s_buf, dp_buf, dk_acc, dv_acc, dq_acc, top, total, weighted,
    *, span, wide,
):
    spans = order_ref.shape[0]
    rows = GROUP * span
    width = wide * span
    tiles = spans // wide + 1
    me = lax.axis_index("ctx")
    first = order_ref[2 * me]
    second = order_ref[2 * me + 1]
    low_half = jnp.where(first < second, 0, 1)
    low = jnp.minimum(first, second)
    high = jnp.maximum(first, second)
    low_tiles = low // wide + 1

    for half in range(2):
        for h in range(GROUP):
            dst = pl.ds(h * span, span)
            src = (pl.ds(half * span, span), pl.ds(h * HEAD_SIZE, HEAD_SIZE))
            qs[half, dst, :] = q_ref[src]
            gs[half, dst, :] = g_ref[src]

    def place(b, _):
        src = pl.ds(pl.multiple_of(b * span, span), span)
        dst = pl.ds(pl.multiple_of(order_ref[b] * span, span), span)
        kseq[dst, :] = k_ref[src, :]
        vseq[dst, :] = v_ref[src, :]
        return 0

    lax.fori_loop(0, spans, place, 0)
    for b in range(spans // wide):
        kt[b] = kseq[pl.ds(b * width, width), :].T

    top[...] = jnp.full_like(top, -1e30)
    total[...] = jnp.zeros_like(total)
    weighted[...] = jnp.zeros_like(weighted)
    dq_acc[...] = jnp.zeros_like(dq_acc)
    dk_acc[...] = jnp.zeros_like(dk_acc)
    dv_acc[...] = jnp.zeros_like(dv_acc)

    def where(t):
        is_low = t < low_tiles
        half = jnp.where(is_low, low_half, 1 - low_half)
        block = jnp.where(is_low, t, t - low_tiles)
        last = jnp.logical_or(t == low_tiles - 1, t == tiles - 1)
        q_span = jnp.where(is_low, low, high)
        return half, block, last, q_span

    def keys_of(ref, block):
        return ref[pl.ds(pl.multiple_of(block * width, width), width), :]

    def score_step(t, _):
        half, block, last, q_span = where(t)
        s_buf[t] = lax.dot_general(
            keys_of(kseq, block), qs[half], NT, preferred_element_type=F32
        )

        @pl.when(last)
        def _():
            key_pos = block * width + lax.broadcasted_iota(jnp.int32, (width, rows), 0)
            q_pos = q_span * span + lax.broadcasted_iota(jnp.int32, (width, rows), 1) % span
            s_buf[t] = jnp.where(key_pos <= q_pos, s_buf[t], -1e30)

        part = jnp.max(s_buf[t].reshape(width // 8, 8, rows), axis=0)
        top[half] = jnp.maximum(top[half], part)
        return 0

    lax.fori_loop(0, tiles, score_step, 0)
    for half in range(2):
        top[half] = jnp.broadcast_to(jnp.max(top[half], axis=0, keepdims=True), (8, rows))

    def exp_step(t, _):
        half, block, _, _ = where(t)
        dp = lax.dot_general(keys_of(vseq, block), gs[half], NT, preferred_element_type=F32)
        e = jnp.exp2((s_buf[t] - top[half][0:1]) * (SCALE * LOG2E))
        s_buf[t] = e
        dp_buf[t] = dp
        total[half] += jnp.sum(e.reshape(width // 8, 8, rows), axis=0)
        weighted[half] += jnp.sum((e * dp).reshape(width // 8, 8, rows), axis=0)
        return 0

    lax.fori_loop(0, tiles, exp_step, 0)
    for half in range(2):
        inverse = 1.0 / jnp.sum(total[half], axis=0, keepdims=True)
        delta = jnp.sum(weighted[half], axis=0, keepdims=True) * inverse
        total[half] = jnp.broadcast_to(inverse, (8, rows))
        weighted[half] = jnp.broadcast_to(delta, (8, rows))

    def grad_step(t, _):
        half, block, _, _ = where(t)
        prob = s_buf[t] * total[half][0:1]
        dscore = (prob * (dp_buf[t] - weighted[half][0:1])).astype(BF16)
        weights = prob.astype(BF16)
        here = pl.ds(pl.multiple_of(block * width, width), width)
        dv_acc[here, :] += jnp.dot(weights, gs[half], preferred_element_type=F32)
        dk_acc[here, :] += jnp.dot(dscore, qs[half], preferred_element_type=F32)
        dq_acc[half] += jnp.dot(kt[block], dscore, preferred_element_type=F32)
        return 0

    lax.fori_loop(0, tiles, grad_step, 0)

    for half in range(2):
        dq = (dq_acc[half] * SCALE).T.astype(BF16)
        for h in range(GROUP):
            dq_ref[pl.ds(half * span, span), pl.ds(h * HEAD_SIZE, HEAD_SIZE)] = dq[
                h * span : (h + 1) * span
            ]

    def put(b, _):
        dst = pl.ds(pl.multiple_of(b * span, span), span)
        src = pl.ds(pl.multiple_of(order_ref[b] * span, span), span)
        dk_ref[dst, :] = (dk_acc[src, :] * SCALE).astype(dk_ref.dtype)
        dv_ref[dst, :] = dv_acc[src, :].astype(dv_ref.dtype)
        return 0

    lax.fori_loop(0, spans, put, 0)


def attention(order, q, g, kv, kv_heads, grad_type):
    tokens, length = q.shape[0], kv.shape[0]
    spans = order.shape[0]
    span = tokens // 2
    rows = GROUP * span
    wide = math.gcd(spans, 4)
    width = wide * span
    tiles = spans // wide + 1
    d = HEAD_SIZE
    elements = kv_heads * tiles * width * rows
    smem = pl.BlockSpec(memory_space=pltpu.SMEM)
    head_block = pl.BlockSpec((tokens, GROUP * d), lambda i: (0, i))
    return pl.pallas_call(
        functools.partial(attention_kernel, span=span, wide=wide),
        grid=(kv_heads,),
        in_specs=[
            smem,
            head_block,
            head_block,
            pl.BlockSpec((length, d), lambda i: (0, i)),
            pl.BlockSpec((length, d), lambda i: (0, i + kv_heads)),
        ],
        out_specs=[
            head_block,
            pl.BlockSpec((length, d), lambda i: (0, i)),
            pl.BlockSpec((length, d), lambda i: (0, i)),
        ],
        out_shape=[
            jax.ShapeDtypeStruct(q.shape, BF16),
            jax.ShapeDtypeStruct((length, kv_heads * d), grad_type),
            jax.ShapeDtypeStruct((length, kv_heads * d), grad_type),
        ],
        scratch_shapes=[
            pltpu.VMEM((2, rows, d), BF16),
            pltpu.VMEM((2, rows, d), BF16),
            pltpu.VMEM((length, d), BF16),
            pltpu.VMEM((length, d), BF16),
            pltpu.VMEM((spans // wide, d, width), BF16),
            pltpu.VMEM((tiles, width, rows), F32),
            pltpu.VMEM((tiles, width, rows), F32),
            pltpu.VMEM((length, d), F32),
            pltpu.VMEM((length, d), F32),
            pltpu.VMEM((2, d, rows), F32),
            pltpu.VMEM((2, 8, rows), F32),
            pltpu.VMEM((2, 8, rows), F32),
            pltpu.VMEM((2, 8, rows), F32),
        ],
        compiler_params=pltpu.CompilerParams(vmem_limit_bytes=48 * 2**20),
        cost_estimate=pl.CostEstimate(
            flops=10 * elements * d, bytes_accessed=8 * 2**20, transcendentals=elements
        ),
        name="attention_grad",
    )(order, q, g, kv, kv)


def body(queries, keys, values, output_gradient, span_order):
    tp = lax.axis_size("tp")
    local = keys.shape[0]
    mine = keys.shape[1] // tp
    kv_heads = mine // HEAD_SIZE
    pair = jnp.stack(
        [keys.reshape(local, tp, mine), values.reshape(local, tp, mine)], axis=2
    ).reshape(local, tp * 2 * mine)
    pair = lax.all_to_all(pair, "tp", split_axis=1, concat_axis=0, tiled=True)
    whole = lax.all_gather(pair, "ctx", axis=0, tiled=True)
    dq, dk, dv = attention(span_order, queries, output_gradient, whole, kv_heads, F32)
    dk = lax.psum_scatter(dk, "ctx", scatter_dimension=0, tiled=True).astype(BF16)
    dv = lax.psum_scatter(dv, "ctx", scatter_dimension=0, tiled=True).astype(BF16)
    both = lax.all_to_all(
        jnp.stack([dk, dv], axis=1), "tp", split_axis=0, concat_axis=2, tiled=True
    )
    return dq, both[:, 0], both[:, 1]


def solution(mesh):
    return jax.shard_map(
        body,
        mesh=mesh,
        in_specs=(
            P("ctx", "tp"),
            P(("ctx", "tp"), None),
            P(("ctx", "tp"), None),
            P("ctx", "tp"),
            P(),
        ),
        out_specs=(P("ctx", "tp"), P(("ctx", "tp"), None), P(("ctx", "tp"), None)),
        check_vma=False,
    )
```

time: 681 us -> 276 us (0.41); the launches traced: 673 us -> 276 us
  local copies, waits for them, and re-layouts: 267 us -> 6.95 us
  matrix products: 151 us -> 0 us
  other arithmetic: 40.5 us -> 2.33 us
  Pallas kernels: 0 us -> 37.6 us
  waiting for transfers between devices: 176 us -> 197 us
    dynamic_update_slice x32 -> x0, local copies, waits for them, and re-layouts: 230 us -> none  [body(): lax.scan(grad_step, start_dq, (k_blocks, v_blocks, pos_blocks))]
    dot_general x64 -> x0, matrix products: 151 us -> none  [the longest x24 46.2 us: scores(): jnp.einsum('gqd,gkd->gqk', q_rows, k_block, preferred_element_type=jnp.fl...]
    pallas_call x0 -> x1, Pallas kernels: none -> 37.6 us  [attention(): pl.pallas_call(functools.partial(attention_kernel, span=span, wide=wide),...]
    mul x1 -> x0, other arithmetic: 15.9 us -> none  [body(): jnp.repeat(span_order, span, total_repeat_length=length) * span]
    unnamed x9 -> x6, local copies, waits for them, and re-layouts: 15.4 us -> 3.1 us
    all_gather x2 -> x1, waiting for transfers between devices: 40.1 us -> 51 us  [body(): whole = lax.all_gather(pair, 'ctx', axis=0, tiled=True)]
    reduce_scatter x2, waiting for transfers between devices: 136 us -> 146 us  [the longest x1 74.7 us: body(): lax.psum_scatter(dv, 'ctx', scatter_dimension=0, tiled=True).astype(BF16)]
    reduce_sum x8 -> x0, other arithmetic: 8.44 us -> none  [stats_step(): total = total * jnp.exp(top - new_top) + jnp.sum(expo, axis=-1)]
  transfers between devices with their start and end apart: 6 -> 3, of which waited for: 4 -> 3; matrix products, arithmetic and copies ran while one was open for 8% -> 0% of each run, Pallas kernels for 0% -> 0%
where the time goes in v1:
time: 276 us
  waiting for transfers between devices  197 us (71%)
  Pallas kernels  37.6 us (14%)
  blocking collectives  17.5 us (6%)
  between operations  13.8 us (5%)
  local copies, waits for them, and re-layouts  6.95 us (3%)
    reduce_scatter x1, waiting for transfers between devices, body(): lax.psum_scatter(dv, 'ctx', scatter_dimension=0, tiled=True).astype(BF16)  74.7 us
    reduce_scatter x1, waiting for transfers between devices, body(): lax.psum_scatter(dk, 'ctx', scatter_dimension=0, tiled=True).astype(BF16)  70.8 us
    all_gather x1, waiting for transfers between devices, body(): whole = lax.all_gather(pair, 'ctx', axis=0, tiled=True)  51 us
    pallas_call x1, Pallas kernels, attention(): pl.pallas_call(functools.partial(attention_kernel, span=span, wide=wide),...  37.6 us
    all_to_all x1, blocking collectives, body(): pair = lax.all_to_all(pair, 'tp', split_axis=1, concat_axis=0, tiled=True)  9.76 us
    all_to_all x1, blocking collectives, body(): lax.all_to_all(jnp.stack([dk, dv], axis=1), 'tp', split_axis=0, concat_ax...  7.74 us
  transfers between devices with their start and end apart: 3, of which 3 were waited for; matrix products, arithmetic and copies ran while one was open for 0% of the time, Pallas kernels for 0%

profile of v1, /device:TPU:0, one launch (start us, length us, event | category | flops | bytes accessed | tf_op | source)
XLA Modules:
  0.0 275.6 jit_solution(10673869717867032103)
XLA Ops:
  7.2 0.0 all-gather.2.cloned.1.call-start
  7.2 1.0 stack_reshape.6
  8.2 1.0 stack_reshape.7
  9.2 0.4 pad_maximum_fusion
  9.6 0.3 copy.10
  9.8 0.2 all_to_all.27
  10.0 9.8 %all_to_all.37 = bf16[64,2,1024]{2,0,1:T(8,128)(2,1)} all-to-all(bf16[64,2,1024]{2,0,1:T(8,128)(2,1)S(1)} %all_to_all.27), channel_id=1, replica_groups=mesh['ctx'=16,'tp'=2] {'tp'}, dimensions={1} | all-to-all | bytes 524288 | tf_op jit(solution)/shard_map/all_to_all | solution.py:205
  19.8 0.0 all-gather.2.cloned.1.call-update
  19.8 0.0 reduce-scatter.3.cloned.1.call-start
  19.9 51.0 %all-gather.2.cloned.1.call-done.k_ref.v_ref = bf16[2048,1024]{1,0:T(8,128)(2,1)} async-done(((bf16[128,1024]{1,0:T(8,128)(2,1)}), bf16[2048,1024]{1,0:T(8,128)(2,1)}) %all-gather.2.cloned.1.call-update) | async-done | bytes 4194320 | tf_op jit(solution)/shard_map/all_gather | solution.py:206
  70.9 0.0 copy-start
  70.9 1.2 copy-done
  72.1 0.0 copy-start.1
  72.1 1.2 copy-done.1
  73.3 0.0 copy-start.2
  73.3 0.7 copy-done.2
  74.0 37.6 %attention_grad.1 = (bf16[128,4096]{1,0:T(8,128)(2,1)}, f32[2048,512]{1,0:T(8,128)}, f32[2048,512]{1,0:T(8,128)}) custom-call(s32[32]{0:T(128)S(1)} %copy-done.2, bf16[128,4096]{1,0:T(8,128)(2,1)S(1)} %copy-done, bf16[128,4096]{1,0:T(8,128)(2,1)S(1)} %copy-done.1, bf16[2048,1024]{1,0:T(8,128)(2,1)} %all-gather.2.cloned.1.call-done.k_ref.v_ref, ...), custom_call_target="tpu_custom_call" | custom-call | flops 6039797760 | bytes 8388608 | tf_op jit(solution)/shard_map/attention_grad/pallas_call | solution.py:154
  111.6 0.0 reduce-scatter.3.cloned.1.call-update
  111.6 0.0 reduce-scatter.5.cloned.1.call-start
  111.7 0.7 reduce-scatter.5.cloned.1.call-update
  112.3 70.8 %reduce-scatter.3.cloned.1.call-done = f32[128,512]{1,0:T(8,128)} async-done(((f32[2048,512]{1,0:T(8,128)}), f32[128,512]{1,0:T(8,128)}) %reduce-scatter.3.cloned.1.call-update) | async-done | bytes 262160 | tf_op jit(solution)/shard_map/reduce_scatter | solution.py:208
  183.1 1.0 convert_bitcast_fusion.1
  184.1 74.7 %reduce-scatter.5.cloned.1.call-done = f32[128,512]{1,0:T(8,128)} async-done(((f32[2048,512]{1,0:T(8,128)}), f32[128,512]{1,0:T(8,128)}) %reduce-scatter.5.cloned.1.call-update) | async-done | bytes 262160 | tf_op jit(solution)/shard_map/reduce_scatter | solution.py:209
  258.8 1.0 convert_bitcast_fusion
  259.9 0.3 copy.11
  260.1 7.7 %all_to_all.38 = bf16[128,2,512]{2,1,0:T(2,128)(2,1)S(1)} all-to-all(bf16[128,2,512]{2,1,0:T(2,128)(2,1)S(1)} %copy.11), channel_id=1, replica_groups=mesh['ctx'=16,'tp'=2] {'tp'}, dimensions={0} | all-to-all | bytes 524288 | tf_op jit(solution)/shard_map/all_to_all | solution.py:210
  267.9 0.3 copy.12
  268.1 0.2 all_to_all.34
  268.3 0.7 slice_bitcast_fusion
  (1 shorter events, 0.0 us)
Async XLA Ops:
  7.2 63.7 %all-gather.2.cloned.1.call-start = ((), (), s32[]{:S(2)}) async-start(), calls=%async_computation.4 | async-start | bytes 4456448 | tf_op jit(solution)/shard_map/all_gather | solution.py:206
  19.8 163.3 %reduce-scatter.3.cloned.1.call-start = ((), (), s32[]{:S(2)}) async-start(), calls=%async_computation.5 | async-start | bytes 4456448 | tf_op jit(solution)/shard_map/reduce_scatter | solution.py:208
  70.9 1.2 copy-start
  72.1 1.2 copy-start.1
  73.3 0.7 copy-start.2
  111.6 147.2 %reduce-scatter.5.cloned.1.call-start = ((), (), s32[]{:S(2)}) async-start(), calls=%async_computation.6 | async-start | bytes 4456448 | tf_op jit(solution)/shard_map/reduce_scatter | solution.py:209
Sparse Core Ops, SparseCore 0:
  19.9 50.9 all-gather.1
  111.7 71.3 reduce-scatter.2
  187.0 71.8 reduce-scatter.4

commit v2 on v1

--- a/solution.py
+++ b/solution.py
@@ -14,13 +14,14 @@
 GROUP = QUERY_HEADS // KEY_VALUE_HEADS
 SCALE = HEAD_SIZE ** (-0.5)
 LOG2E = math.log2(math.e)
+PIECES = 4
 NT = (((1,), (1,)), ((), ()))
 F32 = jnp.float32
 BF16 = jnp.bfloat16
 
 
 def attention_kernel(
-    order_ref, q_ref, g_ref, k_ref, v_ref, dq_ref, dk_ref, dv_ref,
+    order_ref, q_ref, g_ref, k_ref, v_ref, dq_ref, out_ref,
     qs, gs, kseq, vseq, kt, s_buf, dp_buf, dk_acc, dv_acc, dq_acc, top, total, weighted,
     *, span, wide,
 ):
@@ -132,15 +133,16 @@
     def put(b, _):
         dst = pl.ds(pl.multiple_of(b * span, span), span)
         src = pl.ds(pl.multiple_of(order_ref[b] * span, span), span)
-        dk_ref[dst, :] = (dk_acc[src, :] * SCALE).astype(dk_ref.dtype)
-        dv_ref[dst, :] = dv_acc[src, :].astype(dv_ref.dtype)
+        out_ref[0, dst, :] = (dk_acc[src, :] * SCALE).astype(BF16)
+        out_ref[1, dst, :] = dv_acc[src, :].astype(BF16)
         return 0
 
     lax.fori_loop(0, spans, put, 0)
 
 
-def attention(order, q, g, kv, kv_heads, grad_type):
-    tokens, length = q.shape[0], kv.shape[0]
+def attention(order, q, g, kv):
+    tokens, length = q.shape[0], kv.shape[1]
+    kv_heads = kv.shape[2] // HEAD_SIZE
     spans = order.shape[0]
     span = tokens // 2
     rows = GROUP * span
@@ -158,18 +160,16 @@
             smem,
             head_block,
             head_block,
-            pl.BlockSpec((length, d), lambda i: (0, i)),
-            pl.BlockSpec((length, d), lambda i: (0, i + kv_heads)),
+            pl.BlockSpec((None, length, d), lambda i: (0, 0, i)),
+            pl.BlockSpec((None, length, d), lambda i: (1, 0, i)),
         ],
         out_specs=[
             head_block,
-            pl.BlockSpec((length, d), lambda i: (0, i)),
-            pl.BlockSpec((length, d), lambda i: (0, i)),
+            pl.BlockSpec((2, length, d), lambda i: (0, 0, i)),
         ],
         out_shape=[
             jax.ShapeDtypeStruct(q.shape, BF16),
-            jax.ShapeDtypeStruct((length, kv_heads * d), grad_type),
-            jax.ShapeDtypeStruct((length, kv_heads * d), grad_type),
+            jax.ShapeDtypeStruct(kv.shape, BF16),
         ],
         scratch_shapes=[
             pltpu.VMEM((2, rows, d), BF16),
@@ -194,23 +194,308 @@
     )(order, q, g, kv, kv)
 
 
+def ring_place(chips):
+    ctx = lax.axis_index("ctx")
+    chip, core = ctx // 2, ctx % 2
+    depth, column = chip // 2, chip % 2
+    return chip, core, (1 - column) * depth + column * (chips - 1 - depth)
+
+
+def chip_at(position, chips):
+    column = position // (chips // 2)
+    depth = (1 - column) * position + column * (chips - 1 - position)
+    return 2 * depth + column
+
+
+def device(ctx, tp):
+    return dict(device_id=(ctx, tp), device_id_type=pl.DeviceIdType.MESH)
+
+
+def greet(targets):
+    barrier = pltpu.get_barrier_semaphore()
+    for target in targets:
+        pl.semaphore_signal(barrier, inc=1, **target)
+    pl.semaphore_wait(barrier, len(targets))
+
+
+def pieces_of(rows):
+    return math.gcd(rows // 2, PIECES)
+
+
+def gather_kernel(
+    keys_ref, values_ref, out_ref,
+    tp_send, tp_recv, own_sem, pair_send, pair_recv, ring_send, ring_recv, side_send, side_recv,
+    *, chips, tp_size,
+):
+    local, mine = keys_ref.shape[0], out_ref.shape[2]
+    tokens = local * tp_size
+    block = 2 * tokens
+    pieces = pieces_of(block)
+    piece = block // pieces
+    chip, core, position = ring_place(chips)
+    ctx, tp = lax.axis_index("ctx"), lax.axis_index("tp")
+    way = 1 - 2 * core
+    partner = device(2 * chip + 1 - core, tp)
+    ahead = device(2 * chip_at((position + way + chips) % chips, chips) + core, tp)
+    behind = device(2 * chip_at((position - way + chips) % chips, chips) + core, tp)
+    others = [(tp + i) % tp_size for i in range(1, tp_size)]
+    greet([partner, ahead, behind] + [device(ctx, t) for t in others])
+
+    def at(start, size):
+        return pl.ds(pl.multiple_of(start, size), size)
+
+    sources = (keys_ref, values_ref)
+    copies = []
+    landed = at(ctx * tokens + tp * local, local)
+    for a in range(2):
+        for i, t in enumerate(others):
+            copies.append(
+                pltpu.make_async_remote_copy(
+                    src_ref=sources[a].at[:, at(t * mine, mine)],
+                    dst_ref=out_ref.at[a, landed],
+                    send_sem=tp_send.at[a, i],
+                    recv_sem=tp_recv.at[a, i],
+                    **device(ctx, t),
+                )
+            )
+            copies[-1].start()
+    own = []
+    for a in range(2):
+        own.append(
+            pltpu.make_async_copy(
+                sources[a].at[:, at(tp * mine, mine)], out_ref.at[a, landed], own_sem.at[a]
+            )
+        )
+        own[-1].start()
+    for copy in own:
+        copy.wait()
+    for copy in copies:
+        copy.wait()
+
+    pair = []
+    for a in range(2):
+        rows = out_ref.at[a, at(ctx * tokens, tokens)]
+        pair.append(
+            pltpu.make_async_remote_copy(
+                src_ref=rows, dst_ref=rows,
+                send_sem=pair_send.at[a], recv_sem=pair_recv.at[a], **partner,
+            )
+        )
+        pair[-1].start()
+    for copy in pair:
+        copy.wait()
+
+    def ring_copy(step, j):
+        origin = chip_at((position - way * step + 2 * chips * chips) % chips, chips)
+        rows = out_ref.at[core, at(origin * block + j * piece, piece)]
+        return pltpu.make_async_remote_copy(
+            src_ref=rows, dst_ref=rows,
+            send_sem=ring_send.at[step, j], recv_sem=ring_recv.at[step, j], **ahead,
+        )
+
+    def side_copy(step, j):
+        origin = chip_at((position - way * step + 2 * chips * chips) % chips, chips)
+        rows = out_ref.at[core, at(origin * block + j * piece, piece)]
+        return pltpu.make_async_remote_copy(
+            src_ref=rows, dst_ref=rows,
+            send_sem=side_send.at[step - 1, j], recv_sem=side_recv.at[step - 1, j], **partner,
+        )
+
+    for j in range(pieces):
+        ring_copy(0, j).start()
+
+    def forward(step, _):
+        for j in range(pieces):
+            ring_copy(step - 1, j).wait_recv()
+            ring_copy(step, j).start()
+            side_copy(step, j).start()
+        return 0
+
+    lax.fori_loop(1, chips - 1, forward, 0)
+    for j in range(pieces):
+        ring_copy(chips - 2, j).wait_recv()
+        side_copy(chips - 1, j).start()
+
+    def finish(step, _):
+        for j in range(pieces):
+            ring_copy(step - 1, j).wait_send()
+            side_copy(step, j).wait()
+        return 0
+
+    lax.fori_loop(1, chips, finish, 0)
+
+
+def gather(keys, values, ctx_size, tp_size):
+    local, mine = keys.shape[0], keys.shape[1] // tp_size
+    length = local * tp_size * ctx_size
+    chips = ctx_size // 2
+    pieces = pieces_of(2 * local * tp_size)
+    dma = pltpu.SemaphoreType.DMA
+    vmem = pl.BlockSpec(memory_space=pltpu.VMEM)
+    return pl.pallas_call(
+        functools.partial(gather_kernel, chips=chips, tp_size=tp_size),
+        in_specs=[vmem, vmem],
+        out_specs=vmem,
+        out_shape=jax.ShapeDtypeStruct((2, length, mine), BF16),
+        scratch_shapes=[
+            dma((2, tp_size - 1)), dma((2, tp_size - 1)), dma((2,)), dma((2,)), dma((2,)),
+            dma((chips - 1, pieces)), dma((chips - 1, pieces)),
+            dma((chips - 1, pieces)), dma((chips - 1, pieces)),
+        ],
+        compiler_params=pltpu.CompilerParams(collective_id=0, has_side_effects=True),
+        name="gather_pairs",
+    )(keys, values)
+
+
+def scatter_kernel(
+    grads_ref, out_ref, pair_buf, ring_in, ring_out, final,
+    pair_send, pair_recv, ring_send, ring_recv, last_send, last_recv, own_sem,
+    *, chips, tp_size,
+):
+    mine = grads_ref.shape[2]
+    block = grads_ref.shape[1] // chips
+    tokens = block // 2
+    local = tokens // tp_size
+    pieces = pieces_of(block)
+    piece = block // pieces
+    chip, core, position = ring_place(chips)
+    tp = lax.axis_index("tp")
+    way = 1 - 2 * core
+    partner = device(2 * chip + 1 - core, tp)
+    ahead = device(2 * chip_at((position + way + chips) % chips, chips) + core, tp)
+    behind = device(2 * chip_at((position - way + chips) % chips, chips) + core, tp)
+    owners = [
+        (other, (tp + i) % tp_size, other * tp_size + i)
+        for other in range(2)
+        for i in range(tp_size)
+    ]
+    remote = owners[1:]
+    greet(
+        [partner, ahead, behind]
+        + [device(2 * chip + (core + o) % 2, t) for o, t, _ in remote]
+    )
+
+    def at(start, size):
+        return pl.ds(pl.multiple_of(start, size), size)
+
+    def target(step, sign):
+        return chip_at((position - sign * (1 + step) + 2 * chips * chips) % chips, chips)
+
+    def pair_copy(step, j):
+        rows = at(target(step, -way) * block + j * piece, piece)
+        return pltpu.make_async_remote_copy(
+            src_ref=grads_ref.at[1 - core, rows],
+            dst_ref=pair_buf.at[step, at(j * piece, piece)],
+            send_sem=pair_send.at[step, j], recv_sem=pair_recv.at[step, j], **partner,
+        )
+
+    def ring_copy(step, j):
+        rows = at(j * piece, piece)
+        return pltpu.make_async_remote_copy(
+            src_ref=ring_out.at[step, rows],
+            dst_ref=ring_in.at[step, rows],
+            send_sem=ring_send.at[step, j], recv_sem=ring_recv.at[step, j], **ahead,
+        )
+
+    def start_pairs(step, _):
+        for j in range(pieces):
+            pair_copy(step, j).start()
+        return 0
+
+    lax.fori_loop(0, chips, start_pairs, 0)
+
+    def local_terms(step, j):
+        pair_copy(step, j).wait_recv()
+        rows = at(target(step, way) * block + j * piece, piece)
+        theirs = pair_buf[step, pl.ds(j * piece, piece), :].astype(F32)
+        return grads_ref[core, rows, :].astype(F32) + theirs
+
+    for j in range(pieces):
+        ring_out[0, pl.ds(j * piece, piece), :] = local_terms(0, j).astype(BF16)
+        ring_copy(0, j).start()
+
+    def step_body(step, _):
+        for j in range(pieces):
+            terms = local_terms(step, j)
+            ring_copy(step - 1, j).wait_recv()
+            rows = pl.ds(j * piece, piece)
+            arrived = ring_in[step - 1, rows, :].astype(F32)
+            ring_out[step, rows, :] = (terms + arrived).astype(BF16)
+            ring_copy(step, j).start()
+        return 0
+
+    lax.fori_loop(1, chips - 1, step_body, 0)
+    for j in range(pieces):
+        terms = local_terms(chips - 1, j)
+        ring_copy(chips - 2, j).wait_recv()
+        rows = pl.ds(j * piece, piece)
+        final[rows, :] = (terms + ring_in[chips - 2, rows, :].astype(F32)).astype(BF16)
+
+    columns = at(tp * mine, mine)
+    last = []
+    for o, t, sem in remote:
+        who = (core + o) % 2
+        last.append(
+            pltpu.make_async_remote_copy(
+                src_ref=final.at[at(who * tokens + t * local, local)],
+                dst_ref=out_ref.at[core, :, columns],
+                send_sem=last_send.at[sem], recv_sem=last_recv.at[sem],
+                **device(2 * chip + who, t),
+            )
+        )
+        last[-1].start()
+    own = pltpu.make_async_copy(
+        final.at[at(core * tokens + tp * local, local)], out_ref.at[core, :, columns], own_sem
+    )
+    own.start()
+    own.wait()
+    for copy in last:
+        copy.wait()
+
+    def finish(step, _):
+        for j in range(pieces):
+            ring_copy(step, j).wait_send()
+            pair_copy(step, j).wait_send()
+        return 0
+
+    lax.fori_loop(0, chips - 1, finish, 0)
+    for j in range(pieces):
+        pair_copy(chips - 1, j).wait_send()
+
+
+def scatter(grads, ctx_size, tp_size):
+    _, length, mine = grads.shape
+    chips = ctx_size // 2
+    block = length // chips
+    local = block // 2 // tp_size
+    pieces = pieces_of(block)
+    dma = pltpu.SemaphoreType.DMA
+    vmem = pl.BlockSpec(memory_space=pltpu.VMEM)
+    return pl.pallas_call(
+        functools.partial(scatter_kernel, chips=chips, tp_size=tp_size),
+        in_specs=[vmem],
+        out_specs=vmem,
+        out_shape=jax.ShapeDtypeStruct((2, local, mine * tp_size), BF16),
+        scratch_shapes=[
+            pltpu.VMEM((chips, block, mine), BF16),
+            pltpu.VMEM((chips - 1, block, mine), BF16),
+            pltpu.VMEM((chips - 1, block, mine), BF16),
+            pltpu.VMEM((block, mine), BF16),
+            dma((chips, pieces)), dma((chips, pieces)),
+            dma((chips - 1, pieces)), dma((chips - 1, pieces)),
+            dma((2 * tp_size,)), dma((2 * tp_size,)), dma,
+        ],
+        compiler_params=pltpu.CompilerParams(collective_id=1, has_side_effects=True),
+        name="scatter_pairs",
+    )(grads)
+
+
 def body(queries, keys, values, output_gradient, span_order):
-    tp = lax.axis_size("tp")
-    local = keys.shape[0]
-    mine = keys.shape[1] // tp
-    kv_heads = mine // HEAD_SIZE
-    pair = jnp.stack(
-        [keys.reshape(local, tp, mine), values.reshape(local, tp, mine)], axis=2
-    ).reshape(local, tp * 2 * mine)
-    pair = lax.all_to_all(pair, "tp", split_axis=1, concat_axis=0, tiled=True)
-    whole = lax.all_gather(pair, "ctx", axis=0, tiled=True)
-    dq, dk, dv = attention(span_order, queries, output_gradient, whole, kv_heads, F32)
-    dk = lax.psum_scatter(dk, "ctx", scatter_dimension=0, tiled=True).astype(BF16)
-    dv = lax.psum_scatter(dv, "ctx", scatter_dimension=0, tiled=True).astype(BF16)
-    both = lax.all_to_all(
-        jnp.stack([dk, dv], axis=1), "tp", split_axis=0, concat_axis=2, tiled=True
-    )
-    return dq, both[:, 0], both[:, 1]
+    ctx_size, tp_size = lax.axis_size("ctx"), lax.axis_size("tp")
+    kv = gather(keys, values, ctx_size, tp_size)
+    dq, grads = attention(span_order, queries, output_gradient, kv)
+    both = scatter(grads, ctx_size, tp_size)
+    return dq, both[0], both[1]
 
 
 def solution(mesh):

time: 276 us -> 114 us (0.41)
  waiting for transfers between devices: 197 us -> 0 us
  Pallas kernels: 37.6 us -> 111 us
  blocking collectives: 17.5 us -> 0 us
  between operations: 13.8 us -> 0.7 us
  local copies, waits for them, and re-layouts: 6.95 us -> 1.7 us
    reduce_scatter x2 -> x0, waiting for transfers between devices: 146 us -> none  [the longest x1 74.7 us: body(): lax.psum_scatter(dv, 'ctx', scatter_dimension=0, tiled=True).astype(BF16)]
    pallas_call x0 -> x2, Pallas kernels: none -> 74.3 us  [the longest x1 39.6 us: gather(): pl.pallas_call(functools.partial(gather_kernel, chips=chips, tp_size=tp_s...]
    all_gather x1 -> x0, waiting for transfers between devices: 51 us -> none  [body(): whole = lax.all_gather(pair, 'ctx', axis=0, tiled=True)]
    all_to_all x2 -> x0, blocking collectives: 17.5 us -> none  [the longest x1 9.76 us: body(): pair = lax.all_to_all(pair, 'tp', split_axis=1, concat_axis=0, tiled=True)]
    unnamed x6, local copies, waits for them, and re-layouts: 3.1 us -> 0.01 us
  transfers between devices with their start and end apart: 3 -> 0, of which waited for: 3 -> 0; matrix products, arithmetic and copies ran while one was open for 0% -> 0% of each run, Pallas kernels for 0% -> 0%
where the time goes in v2:
time: 114 us
  Pallas kernels  111 us (97%)
  local copies, waits for them, and re-layouts  1.7 us (1%)
    pallas_call x1, Pallas kernels, gather(): pl.pallas_call(functools.partial(gather_kernel, chips=chips, tp_size=tp_s...  39.6 us
    pallas_call x1, Pallas kernels, attention(): pl.pallas_call(functools.partial(attention_kernel, span=span, wide=wide),...  37.2 us
    pallas_call x1, Pallas kernels, scatter(): pl.pallas_call(functools.partial(scatter_kernel, chips=chips, tp_size=tp_...  34.7 us

profile of v2, /device:TPU:0, one launch (start us, length us, event | category | flops | bytes accessed | tf_op | source)
XLA Modules:
  0.0 113.9 jit_solution(12891804129008027725)
XLA Ops:
  0.6 0.0 copy-start.2
  0.6 0.0 copy-start.1
  0.7 0.0 copy-start
  0.7 39.6 %gather_pairs.1.k_ref.v_ref = bf16[2,2048,512]{2,1,0:T(8,128)(2,1)} custom-call(bf16[64,1024]{1,0:T(8,128)(2,1)} %keys_ref.1, bf16[64,1024]{1,0:T(8,128)(2,1)} %values_ref.1), custom_call_target="tpu_custom_call" | custom-call | tf_op jit(solution)/shard_map/gather_pairs/pallas_call | solution.py:335
  40.3 0.0 copy-done.2
  40.3 0.0 copy-done.1
  40.3 0.0 copy-done
  40.3 37.2 %attention_grad.1 = (bf16[128,4096]{1,0:T(8,128)(2,1)}, bf16[2,2048,512]{2,1,0:T(8,128)(2,1)}) custom-call(s32[32]{0:T(128)S(1)} %copy-done.2, bf16[128,4096]{1,0:T(8,128)(2,1)S(1)} %copy-done, bf16[128,4096]{1,0:T(8,128)(2,1)S(1)} %copy-done.1, bf16[2,2048,512]{2,1,0:T(8,128)(2,1)} %gather_pairs.1.k_ref.v_ref, bf16[2,2048,512]{2,1,0:T(8,128)(2,1)} %gather_pairs.1.k_ref.v_ref), custom_call_target="tpu_custom_call" | custom-call | flops 6039797760 | bytes 8388608 | tf_op jit(solution)/shard_map/attention_grad/pallas_call | solution.py:156
  77.5 34.7 %scatter_pairs.1 = bf16[2,64,1024]{2,1,0:T(8,128)(2,1)} custom-call(bf16[2,2048,512]{2,1,0:T(8,128)(2,1)} %get-tuple-element.6.grads_ref), custom_call_target="tpu_custom_call" | custom-call | tf_op jit(solution)/shard_map/scatter_pairs/pallas_call | solution.py:474
  112.2 1.7 %slice_bitcast_fusion = (bf16[64,1024]{1,0:T(8,128)(2,1)}, bf16[64,1024]{1,0:T(8,128)(2,1)}) fusion(bf16[2,64,1024]{2,1,0:T(8,128)(2,1)} %scatter_pairs.1), kind=kLoop, calls=%fused_computation | loop fusion | bytes 524288 | tf_op jit(solution)/shard_map/squeeze | solution.py:498
Async XLA Ops:
  0.6 39.7 %copy-start.2 = (s32[32]{0:T(128)S(1)}, s32[32]{0:T(128)}, u32[]{:S(2)}) copy-start(s32[32]{0:T(128)} %order_ref.1) | copy-start | bytes 388
  0.6 39.7 %copy-start.1 = (bf16[128,4096]{1,0:T(8,128)(2,1)S(1)}, bf16[128,4096]{1,0:T(8,128)(2,1)}, u32[]{:S(2)}) copy-start(bf16[128,4096]{1,0:T(8,128)(2,1)} %g_ref.1) | copy-start | bytes 3145732
  0.7 39.7 %copy-start = (bf16[128,4096]{1,0:T(8,128)(2,1)S(1)}, bf16[128,4096]{1,0:T(8,128)(2,1)}, u32[]{:S(2)}) copy-start(bf16[128,4096]{1,0:T(8,128)(2,1)} %q_ref.1) | copy-start | bytes 3145732

commit v3 on v2

--- a/solution.py
+++ b/solution.py
@@ -14,7 +14,8 @@
 GROUP = QUERY_HEADS // KEY_VALUE_HEADS
 SCALE = HEAD_SIZE ** (-0.5)
 LOG2E = math.log2(math.e)
-PIECES = 4
+PIECES = 8
+UNROLL = 9
 NT = (((1,), (1,)), ((), ()))
 F32 = jnp.float32
 BF16 = jnp.bfloat16
@@ -73,27 +74,38 @@
     def keys_of(ref, block):
         return ref[pl.ds(pl.multiple_of(block * width, width), width), :]
 
-    def score_step(t, _):
-        half, block, last, q_span = where(t)
-        s_buf[t] = lax.dot_general(
-            keys_of(kseq, block), qs[half], NT, preferred_element_type=F32
-        )
-
-        @pl.when(last)
-        def _():
-            key_pos = block * width + lax.broadcasted_iota(jnp.int32, (width, rows), 0)
-            q_pos = q_span * span + lax.broadcasted_iota(jnp.int32, (width, rows), 1) % span
-            s_buf[t] = jnp.where(key_pos <= q_pos, s_buf[t], -1e30)
-
-        part = jnp.max(s_buf[t].reshape(width // 8, 8, rows), axis=0)
-        top[half] = jnp.maximum(top[half], part)
-        return 0
-
-    lax.fori_loop(0, tiles, score_step, 0)
+    def sweep(step):
+        def several(i, _):
+            for u in range(UNROLL):
+                step(i * UNROLL + u)
+            return 0
+
+        lax.fori_loop(0, tiles // UNROLL, several, 0)
+        for t in range(tiles // UNROLL * UNROLL, tiles):
+            step(t)
+
+    def raise_top(half, score, skip):
+        part = jnp.max(score.reshape(width // 8, 8, rows), axis=0)
+        top[half] = jnp.maximum(top[half], jnp.where(skip, -1e30, part))
+
+    def score_step(t):
+        half, block, last, _ = where(t)
+        score = lax.dot_general(keys_of(kseq, block), qs[half], NT, preferred_element_type=F32)
+        s_buf[t] = score
+        raise_top(half, score, last)
+
+    sweep(score_step)
+    for t in (low_tiles - 1, tiles - 1):
+        half, block, _, q_span = where(t)
+        key_pos = block * width + lax.broadcasted_iota(jnp.int32, (width, rows), 0)
+        q_pos = q_span * span + lax.broadcasted_iota(jnp.int32, (width, rows), 1) % span
+        score = jnp.where(key_pos <= q_pos, s_buf[t], -1e30)
+        s_buf[t] = score
+        raise_top(half, score, False)
     for half in range(2):
         top[half] = jnp.broadcast_to(jnp.max(top[half], axis=0, keepdims=True), (8, rows))
 
-    def exp_step(t, _):
+    def exp_step(t):
         half, block, _, _ = where(t)
         dp = lax.dot_general(keys_of(vseq, block), gs[half], NT, preferred_element_type=F32)
         e = jnp.exp2((s_buf[t] - top[half][0:1]) * (SCALE * LOG2E))
@@ -101,16 +113,15 @@
         dp_buf[t] = dp
         total[half] += jnp.sum(e.reshape(width // 8, 8, rows), axis=0)
         weighted[half] += jnp.sum((e * dp).reshape(width // 8, 8, rows), axis=0)
-        return 0
-
-    lax.fori_loop(0, tiles, exp_step, 0)
+
+    sweep(exp_step)
     for half in range(2):
         inverse = 1.0 / jnp.sum(total[half], axis=0, keepdims=True)
         delta = jnp.sum(weighted[half], axis=0, keepdims=True) * inverse
         total[half] = jnp.broadcast_to(inverse, (8, rows))
         weighted[half] = jnp.broadcast_to(delta, (8, rows))
 
-    def grad_step(t, _):
+    def grad_step(t):
         half, block, _, _ = where(t)
         prob = s_buf[t] * total[half][0:1]
         dscore = (prob * (dp_buf[t] - weighted[half][0:1])).astype(BF16)
@@ -119,9 +130,8 @@
         dv_acc[here, :] += jnp.dot(weights, gs[half], preferred_element_type=F32)
         dk_acc[here, :] += jnp.dot(dscore, qs[half], preferred_element_type=F32)
         dq_acc[half] += jnp.dot(kt[block], dscore, preferred_element_type=F32)
-        return 0
-
-    lax.fori_loop(0, tiles, grad_step, 0)
+
+    sweep(grad_step)
 
     for half in range(2):
         dq = (dq_acc[half] * SCALE).T.astype(BF16)
@@ -267,10 +277,36 @@
             )
         )
         own[-1].start()
+    half = pieces // 2
+    early = local // piece if local % piece == 0 else 0
+
+    def rows_of(step, j):
+        origin = chip_at((position - way * step + 2 * chips * chips) % chips, chips)
+        inside = ((tp * local) // piece * piece + (j % half) * piece) % tokens
+        return at(origin * block + ((core + j // half) % 2) * tokens + inside, piece)
+
+    def ring_copy(step, j):
+        rows = out_ref.at[core, rows_of(step, j)]
+        return pltpu.make_async_remote_copy(
+            src_ref=rows, dst_ref=rows,
+            send_sem=ring_send.at[step, j], recv_sem=ring_recv.at[step, j], **ahead,
+        )
+
+    def side_copy(step, j):
+        rows = out_ref.at[core, rows_of(step, j)]
+        return pltpu.make_async_remote_copy(
+            src_ref=rows, dst_ref=rows,
+            send_sem=side_send.at[step - 1, j], recv_sem=side_recv.at[step - 1, j], **partner,
+        )
+
     for copy in own:
         copy.wait()
+    for j in range(early):
+        ring_copy(0, j).start()
     for copy in copies:
         copy.wait()
+    for j in range(early, half):
+        ring_copy(0, j).start()
 
     pair = []
     for a in range(2):
@@ -284,24 +320,7 @@
         pair[-1].start()
     for copy in pair:
         copy.wait()
-
-    def ring_copy(step, j):
-        origin = chip_at((position - way * step + 2 * chips * chips) % chips, chips)
-        rows = out_ref.at[core, at(origin * block + j * piece, piece)]
-        return pltpu.make_async_remote_copy(
-            src_ref=rows, dst_ref=rows,
-            send_sem=ring_send.at[step, j], recv_sem=ring_recv.at[step, j], **ahead,
-        )
-
-    def side_copy(step, j):
-        origin = chip_at((position - way * step + 2 * chips * chips) % chips, chips)
-        rows = out_ref.at[core, at(origin * block + j * piece, piece)]
-        return pltpu.make_async_remote_copy(
-            src_ref=rows, dst_ref=rows,
-            send_sem=side_send.at[step - 1, j], recv_sem=side_recv.at[step - 1, j], **partner,
-        )
-
-    for j in range(pieces):
+    for j in range(half, pieces):
         ring_copy(0, j).start()
 
     def forward(step, _):

time: 114 us -> 98.6 us (0.86)
  Pallas kernels: 111 us -> 96 us
    pallas_call x1, Pallas kernels: 37.2 us -> 24.9 us  [attention(): pl.pallas_call(functools.partial(attention_kernel, span=span, wide=wide),...]
    pallas_call x1, Pallas kernels: 39.6 us -> 37.8 us  [gather(): pl.pallas_call(functools.partial(gather_kernel, chips=chips, tp_size=tp_s...]
    pallas_call x1, Pallas kernels: 34.7 us -> 33.3 us  [scatter(): pl.pallas_call(functools.partial(scatter_kernel, chips=chips, tp_size=tp_...]
where the time goes in v3:
time: 98.6 us; the launch traced here: 98.4 us
  Pallas kernels  96 us (97%)
  local copies, waits for them, and re-layouts  1.7 us (2%)
    pallas_call x1, Pallas kernels, gather(): pl.pallas_call(functools.partial(gather_kernel, chips=chips, tp_size=tp_s...  37.8 us
    pallas_call x1, Pallas kernels, scatter(): pl.pallas_call(functools.partial(scatter_kernel, chips=chips, tp_size=tp_...  33.3 us
    pallas_call x1, Pallas kernels, attention(): pl.pallas_call(functools.partial(attention_kernel, span=span, wide=wide),...  24.9 us

profile of v3, /device:TPU:0, one launch (start us, length us, event | category | flops | bytes accessed | tf_op | source)
XLA Modules:
  0.0 98.4 jit_solution(13946024367955349379)
XLA Ops:
  0.6 0.0 copy-start.2
  0.6 0.0 copy-start.1
  0.7 0.0 copy-start
  0.7 37.8 %gather_pairs.1.k_ref.v_ref = bf16[2,2048,512]{2,1,0:T(8,128)(2,1)} custom-call(bf16[64,1024]{1,0:T(8,128)(2,1)} %keys_ref.1, bf16[64,1024]{1,0:T(8,128)(2,1)} %values_ref.1), custom_call_target="tpu_custom_call" | custom-call | tf_op jit(solution)/shard_map/gather_pairs/pallas_call | solution.py:354
  38.4 0.0 copy-done.2
  38.5 0.0 copy-done.1
  38.5 0.0 copy-done
  38.5 24.9 %attention_grad.1 = (bf16[128,4096]{1,0:T(8,128)(2,1)}, bf16[2,2048,512]{2,1,0:T(8,128)(2,1)}) custom-call(s32[32]{0:T(128)S(1)} %copy-done.2, bf16[128,4096]{1,0:T(8,128)(2,1)S(1)} %copy-done, bf16[128,4096]{1,0:T(8,128)(2,1)S(1)} %copy-done.1, bf16[2,2048,512]{2,1,0:T(8,128)(2,1)} %gather_pairs.1.k_ref.v_ref, bf16[2,2048,512]{2,1,0:T(8,128)(2,1)} %gather_pairs.1.k_ref.v_ref), custom_call_target="tpu_custom_call" | custom-call | flops 6039797760 | bytes 8388608 | tf_op jit(solution)/shard_map/attention_grad/pallas_call | solution.py:166
  63.4 33.3 %scatter_pairs.1 = bf16[2,64,1024]{2,1,0:T(8,128)(2,1)} custom-call(bf16[2,2048,512]{2,1,0:T(8,128)(2,1)} %get-tuple-element.6.grads_ref), custom_call_target="tpu_custom_call" | custom-call | tf_op jit(solution)/shard_map/scatter_pairs/pallas_call | solution.py:493
  96.7 1.7 %slice_bitcast_fusion = (bf16[64,1024]{1,0:T(8,128)(2,1)}, bf16[64,1024]{1,0:T(8,128)(2,1)}) fusion(bf16[2,64,1024]{2,1,0:T(8,128)(2,1)} %scatter_pairs.1), kind=kLoop, calls=%fused_computation | loop fusion | bytes 524288 | tf_op jit(solution)/shard_map/squeeze | solution.py:517
Async XLA Ops:
  0.6 37.8 %copy-start.2 = (s32[32]{0:T(128)S(1)}, s32[32]{0:T(128)}, u32[]{:S(2)}) copy-start(s32[32]{0:T(128)} %order_ref.1) | copy-start | bytes 388
  0.6 37.8 %copy-start.1 = (bf16[128,4096]{1,0:T(8,128)(2,1)S(1)}, bf16[128,4096]{1,0:T(8,128)(2,1)}, u32[]{:S(2)}) copy-start(bf16[128,4096]{1,0:T(8,128)(2,1)} %g_ref.1) | copy-start | bytes 3145732
  0.7 37.8 %copy-start = (bf16[128,4096]{1,0:T(8,128)(2,1)S(1)}, bf16[128,4096]{1,0:T(8,128)(2,1)}, u32[]{:S(2)}) copy-start(bf16[128,4096]{1,0:T(8,128)(2,1)} %q_ref.1) | copy-start | bytes 3145732
